TPU v7x, 32 devices: a whole 2x2x4 slice. The times are simulated.
32 devices in a mesh: frame: 16 (over z, y, core), stream: 2 (over x).
Axes of the slice: x: 2, y: 2, z: 4, core: 2. Of those that a mesh axis runs over, the one named last changes fastest.
Arguments:
- query: bfloat16 [2, 2048, 4096], P('stream', 'frame'), may hold values from -60 to 60
- key: bfloat16 [2, 2048, 4096], P('stream', 'frame'), may hold values from -4 to 4
- value: bfloat16 [2, 2048, 4096], P('stream', 'frame'), may hold values from -24 to 24
- latent: bfloat16 [2, 2048, 4096], P('stream', 'frame'), may hold values from -6 to 6
- target: bfloat16 [2, 2048, 4096], P('stream', 'frame'), may hold values from -6 to 6
- noise_level: float32 [2, 16], P('stream'), may hold values from 0.02 to 0.98
- mod_weight: bfloat16 [4096, 256], replicated, may hold values from -0.375 to 0.375
- block_order: int32 [32], replicated, may hold values from 0 to 31, as said below
- context_start: int32 [2, 16], P('stream'), may hold values from 0 to 15, as said below
Outputs:
- grad_weight: float32 [4096, 256], P('frame')
Inputs may be any that keep to these rules, and one draw needn't show every extreme that they name: block_order is a permutation of 0 to 31, and entries 2 i and 2 i + 1 add up to 31. context_start[s, c] lies between 0 and c.
All inputs are finite; a program needn't handle non-finite values.
Results may differ from a plain program's by a relative error of at most 0.0016.
Values may be sent and summed in bfloat16 or wider, within the bound.
A program may use at most 64 MiB of HBM per device.

v0:
```python
import functools
import math

import jax
import jax.numpy as jnp
from jax import lax
from jax.experimental import pallas as pl
from jax.experimental.pallas import tpu as pltpu
from jax.sharding import PartitionSpec as P

HEAD_DIM = 128
HIDDEN = -1e30


def sinusoid(noise, emb_width):
    half_width = emb_width // 2
    frequency = jnp.exp(-math.log(10000.0) * jnp.arange(half_width, dtype=jnp.float32) / half_width)
    angles = 1000.0 * noise[..., None] * frequency
    return jnp.concatenate([jnp.cos(angles), jnp.sin(angles)], -1).astype(jnp.bfloat16)


def kernel(
    frames,
    streams,
    order_ref,
    start_ref,
    embed_ref,
    query_ref,
    key_ref,
    value_ref,
    latent_ref,
    target_ref,
    weight_ref,
    out_ref,
    query_in,
    key_in,
    value_in,
    diff_in,
    key_sorted,
    value_sorted,
    attn_all,
    latent_own,
    target_own,
    diff_own,
    weight_own,
    embed_all,
    sums_all,
    squares,
    place,
    send_sems,
    recv_sems,
    side_send,
    side_recv,
    local_sems,
):
    me = lax.axis_index("frame")
    my_stream = lax.axis_index("stream")
    own, block_len, width = query_ref.shape
    local = width // frames
    blocks = query_in.shape[0]
    groups = embed_ref.shape[0]
    per_group = blocks // groups
    group_len = per_group * block_len
    seq_len = blocks * block_len
    heads = local // HEAD_DIM

    def peer_of(i):
        return lax.rem(me + i // 2 + lax.rem(i, 2) * (frames // 2), frames)

    barrier = pltpu.get_barrier_semaphore()

    @pl.loop(1, frames)
    def _(i):
        pl.semaphore_signal(barrier, inc=1, device_id={"frame": peer_of(i)})

    for i in range(1, streams):
        pl.semaphore_signal(
            barrier, inc=1, device_id={"stream": lax.rem(my_stream + i, streams)}
        )

    early = (
        pltpu.make_async_copy(latent_ref, latent_own, local_sems.at[0]),
        pltpu.make_async_copy(target_ref, target_own, local_sems.at[1]),
        pltpu.make_async_copy(
            weight_ref.at[pl.ds(me * local, local), :], weight_own, local_sems.at[2]
        ),
    )
    mine = tuple(
        pltpu.make_async_copy(
            source.at[:, :, pl.ds(me * local, local)],
            landing.at[pl.ds(me * own, own)],
            local_sems.at[3 + number],
        )
        for number, (source, landing) in enumerate(
            ((key_ref, key_in), (query_ref, query_in), (value_ref, value_in))
        )
    )
    for copy in early + mine:
        copy.start()
    pl.semaphore_wait(barrier, frames - 1 + streams - 1)

    def sending(number, source, landing, peer):
        return pltpu.make_async_remote_copy(
            src_ref=source.at[:, :, pl.ds(pl.multiple_of(peer * local, local), local)],
            dst_ref=landing.at[pl.ds(me * own, own)],
            send_sem=send_sems.at[number, peer],
            recv_sem=recv_sems.at[number, me],
            device_id={"frame": peer},
        )

    def arriving(number, source, landing, peer):
        return pltpu.make_async_remote_copy(
            src_ref=source.at[:, :, pl.ds(pl.multiple_of(peer * local, local), local)],
            dst_ref=landing.at[pl.ds(peer * own, own)],
            send_sem=send_sems.at[number, peer],
            recv_sem=recv_sems.at[number, peer],
            device_id={"frame": peer},
        )

    def send_all(number, source, landing):
        @pl.loop(1, frames)
        def _(i):
            sending(number, source, landing, peer_of(i)).start()

    def await_all(number, source, landing):
        @pl.loop(1, frames)
        def _(i):
            arriving(number, source, landing, peer_of(i)).wait()

    send_all(0, key_ref, key_in)
    send_all(1, query_ref, query_in)
    send_all(2, value_ref, value_in)

    def side_copies(part, source, landing):
        return [
            pltpu.make_async_remote_copy(
                src_ref=source,
                dst_ref=landing.at[my_stream],
                send_sem=side_send.at[part, i],
                recv_sem=side_recv.at[part, i],
                device_id={"stream": lax.rem(my_stream + i, streams)},
            )
            for i in range(1, streams)
        ]

    embed_copies = side_copies(0, embed_ref, embed_all)
    for copy in embed_copies:
        copy.start()
    embed_all[my_stream] = embed_ref[...]

    for copy in early:
        copy.wait()

    @pl.loop(0, frames)
    def _(i):
        columns = pl.ds(pl.multiple_of(i * local, local), local)
        for b in range(own):
            diff_own[b, :, columns] = (
                latent_own[b, :, columns].astype(jnp.float32)
                - target_own[b, :, columns].astype(jnp.float32)
            ).astype(jnp.bfloat16)

    my_diff = pltpu.make_async_copy(
        diff_own.at[:, :, pl.ds(me * local, local)],
        diff_in.at[pl.ds(me * own, own)],
        local_sems.at[6],
    )
    send_all(3, diff_own, diff_in)
    my_diff.start()

    gate = lax.dot_general(
        embed_ref[...].astype(jnp.bfloat16),
        weight_own[...],
        (((1,), (1,)), ((), ())),
        preferred_element_type=jnp.float32,
    )

    @pl.loop(0, blocks)
    def _(t):
        found = jnp.int32(0)
        for b in range(blocks):
            found = jnp.where(order_ref[b] == t, b, found)
        place[t] = found

    for copy in mine:
        copy.wait()
    await_all(0, key_ref, key_in)

    @pl.loop(0, blocks)
    def _(t):
        rows = pl.ds(pl.multiple_of(t * block_len, block_len), block_len)
        key_sorted[rows, :] = key_in[place[t]]

    await_all(1, query_ref, query_in)
    await_all(2, value_ref, value_in)

    @pl.loop(0, blocks)
    def _(t):
        rows = pl.ds(pl.multiple_of(t * block_len, block_len), block_len)
        value_sorted[rows, :] = value_in[place[t]]

    factor = math.log2(math.e) / math.sqrt(HEAD_DIM)

    def gathered(source, c):
        return jnp.concatenate(
            [source[place[c * per_group + i]] for i in range(per_group)], axis=0
        )

    ranges = math.gcd(groups, 4)
    for number in range(ranges):
        length = (number + 1) * (seq_len // ranges)

        @pl.loop(number * (groups // ranges), (number + 1) * (groups // ranges))
        def _(c):
            rows = gathered(query_in, c)
            column_group = lax.broadcasted_iota(jnp.int32, (1, length), 1) // group_len
            bias = jnp.where(
                (column_group >= start_ref[c]) & (column_group <= c), 0.0, HIDDEN
            ).astype(jnp.float32)
            parts = []
            for h in range(heads):
                lanes = slice(h * HEAD_DIM, (h + 1) * HEAD_DIM)
                scores = (
                    lax.dot_general(
                        rows[:, lanes],
                        key_sorted[:length, lanes],
                        (((1,), (1,)), ((), ())),
                        preferred_element_type=jnp.float32,
                    )
                    + bias
                )
                peak = jnp.max(scores, axis=-1, keepdims=True)
                unnorm = jnp.exp2((scores - peak) * factor)
                inverse = 1.0 / jnp.sum(unnorm, axis=-1, keepdims=True)
                probs = (unnorm * inverse).astype(jnp.bfloat16)
                parts.append(
                    lax.dot_general(
                        probs,
                        value_sorted[:length, lanes],
                        (((1,), (0,)), ((), ())),
                        preferred_element_type=jnp.float32,
                    ).astype(jnp.bfloat16)
                )
            attn = jnp.concatenate(parts, axis=1)
            attn_all[c] = attn
            wide = attn.astype(jnp.float32)
            squares[pl.ds(c, 1), :] = jnp.sum(wide * wide, axis=0, keepdims=True)

    my_diff.wait()
    await_all(3, diff_own, diff_in)

    @pl.loop(0, groups)
    def _(c):
        product = attn_all[c].astype(jnp.float32) * gathered(diff_in, c).astype(jnp.float32)
        sums_all[my_stream, pl.ds(c, 1), :] = jnp.sum(product, axis=0, keepdims=True)

    sums_all[my_stream] = sums_all[my_stream] + gate * squares[...]
    sum_copies = side_copies(1, sums_all.at[my_stream], sums_all)
    for copy in sum_copies:
        copy.start()
    for copy in embed_copies:
        copy.wait()
    for copy in sum_copies:
        copy.wait()
    out_ref[...] = lax.dot_general(
        sums_all[...].reshape(streams * groups, local),
        embed_all[...].reshape(streams * groups, embed_ref.shape[1]),
        (((0,), (0,)), ((), ())),
        precision=lax.Precision.HIGHEST,
        preferred_element_type=jnp.float32,
    ) * (1.0 / math.sqrt(group_len))


def per_device(
    query, key, value, latent, target, noise_level, mod_weight, block_order, context_start
):
    frames = lax.axis_size("frame")
    streams = lax.axis_size("stream")
    tokens, width = query.shape[1:]
    local = width // frames
    blocks = block_order.shape[0]
    own = blocks // frames
    block_len = tokens // own
    groups = noise_level.shape[1]
    emb_width = mod_weight.shape[1]
    group_len = blocks // groups * block_len
    seq_len = blocks * block_len
    embed = sinusoid(noise_level[0], emb_width).astype(jnp.float32)
    bf16, f32 = jnp.bfloat16, jnp.float32
    shaped = [x.reshape(own, block_len, width) for x in (query, key, value, latent, target)]
    anywhere = pl.BlockSpec(memory_space=pl.ANY)
    scalars = pl.BlockSpec(memory_space=pltpu.SMEM)
    vectors = pl.BlockSpec(memory_space=pltpu.VMEM)
    landing = pltpu.VMEM((blocks, block_len, local), bf16)
    ordered = pltpu.VMEM((seq_len, local), bf16)
    held = pltpu.VMEM((own, block_len, width), bf16)
    return pl.pallas_call(
        functools.partial(kernel, frames, streams),
        out_shape=jax.ShapeDtypeStruct((local, emb_width), f32),
        in_specs=[scalars, scalars, vectors] + [anywhere] * 6,
        out_specs=vectors,
        scratch_shapes=[
            landing,
            landing,
            landing,
            landing,
            ordered,
            ordered,
            pltpu.VMEM((groups, group_len, local), bf16),
            held,
            held,
            held,
            pltpu.VMEM((local, emb_width), bf16),
            pltpu.VMEM((streams, groups, emb_width), f32),
            pltpu.VMEM((streams, groups, local), f32),
            pltpu.VMEM((groups, local), f32),
            pltpu.SMEM((blocks,), jnp.int32),
            pltpu.SemaphoreType.DMA((4, frames)),
            pltpu.SemaphoreType.DMA((4, frames)),
            pltpu.SemaphoreType.DMA((2, streams)),
            pltpu.SemaphoreType.DMA((2, streams)),
            pltpu.SemaphoreType.DMA((7,)),
        ],
        compiler_params=pltpu.CompilerParams(
            collective_id=0, has_side_effects=True, vmem_limit_bytes=56 * 1024 * 1024
        ),
    )(block_order, context_start[0], embed, *shaped, mod_weight)


def solution(mesh):
    placed = (
        P("stream", "frame", None),
        P("stream", "frame", None),
        P("stream", "frame", None),
        P("stream", "frame", None),
        P("stream", "frame", None),
        P("stream", None),
        P(),
        P(),
        P("stream", None),
    )
    return jax.shard_map(
        per_device, mesh=mesh, in_specs=placed, out_specs=P("frame", None), check_vma=False
    )
```

profile of v0, /device:TPU:0, one launch (start us, length us, event | category | flops | bytes accessed | tf_op | source)
XLA Modules:
  0.0 116.0 jit_solution(6214016967768818202)
XLA Ops:
  0.0 0.7 multiply_bitcast_fusion
  0.7 0.1 fusion
  0.8 0.6 maximum_convert_fusion.embed_ref
  1.4 112.9 %shard_map.91 = f32[256,256]{1,0:T(8,128)} custom-call(s32[32]{0:T(128)} %order_ref.1, s32[16]{0:T(128)} %bitcast.13, f32[16,256]{1,0:T(8,128)} %maximum_convert_fusion.embed_ref, bf16[2,64,4096]{2,1,0:T(8,128)(2,1)} %bitcast.8, bf16[2,64,4096]{2,1,0:T(8,128)(2,1)} %bitcast.9, bf16[2,64,4096]{2,1,0:T(8,128)(2,1)} %bitcast.10, bf16[2,64,4096]{2,1,0:T(8,128)(2,1)} %bitcast.11, ...), custom_call_target="tpu_custom_call" | custom-call | tf_op jit(solution)/shard_map/pallas_call | solution.py:297
  114.3 1.7 %copy.11 = f32[256,256]{1,0:T(8,128)} copy(f32[256,256]{1,0:T(8,128)} %shard_map.91) | data formatting | bytes 524288
  (1 shorter events, 0.0 us)
where the time goes:
time: 116 us
  Pallas kernels  113 us (97%)
  local copies, waits for them, and re-layouts  1.67 us (1%)
  other arithmetic  1.4 us (1%)
    pallas_call x1, Pallas kernels, per_device(): pl.pallas_call(functools.partial(kernel, frames, streams), out_shape=jax....  113 us

commit v1 on v0

v1 whole, which is shorter than its diff:
```python
import functools
import math

import jax
import jax.numpy as jnp
from jax import lax
from jax.experimental import pallas as pl
from jax.experimental.pallas import tpu as pltpu
from jax.sharding import PartitionSpec as P

HEAD_DIM = 128
HIDDEN = -1e30


def sinusoid(noise, emb_width):
    half_width = emb_width // 2
    frequency = jnp.exp(-math.log(10000.0) * jnp.arange(half_width, dtype=jnp.float32) / half_width)
    angles = 1000.0 * noise[..., None] * frequency
    return jnp.concatenate([jnp.cos(angles), jnp.sin(angles)], -1).astype(jnp.bfloat16)


def kernel(
    frames,
    streams,
    order_ref,
    start_ref,
    embed_ref,
    query_ref,
    key_ref,
    value_ref,
    latent_ref,
    target_ref,
    weight_ref,
    out_ref,
    query_in,
    key_in,
    value_in,
    diff_in,
    key_sorted,
    value_sorted,
    attn_all,
    latent_own,
    target_own,
    diff_own,
    weight_own,
    embed_all,
    sums_all,
    squares,
    base,
    partial,
    place,
    send_sems,
    recv_sems,
    side_send,
    side_recv,
    local_sems,
):
    me = lax.axis_index("frame")
    my_stream = lax.axis_index("stream")
    own, block_len, width = query_ref.shape
    local = width // frames
    blocks = diff_in.shape[0]
    groups = embed_ref.shape[0]
    per_group = blocks // groups
    group_len = per_group * block_len
    seq_len = blocks * block_len
    heads = local // HEAD_DIM

    barrier = pltpu.get_barrier_semaphore()

    @pl.loop(1, frames)
    def _(i):
        pl.semaphore_signal(barrier, inc=1, device_id={"frame": lax.rem(me + i, frames)})

    for i in range(1, streams):
        pl.semaphore_signal(
            barrier, inc=1, device_id={"stream": lax.rem(my_stream + i, streams)}
        )

    early = (
        pltpu.make_async_copy(latent_ref, latent_own, local_sems.at[0]),
        pltpu.make_async_copy(target_ref, target_own, local_sems.at[1]),
        pltpu.make_async_copy(
            weight_ref.at[pl.ds(me * local, local), :], weight_own, local_sems.at[2]
        ),
    )
    moved = ((key_ref, key_in), (query_ref, query_in), (value_ref, value_in))
    mine = tuple(
        pltpu.make_async_copy(
            source.at[:, :, pl.ds(pl.multiple_of(me * local + h * HEAD_DIM, HEAD_DIM), HEAD_DIM)],
            landing[h].at[pl.ds(me * own, own)],
            local_sems.at[4 + h * len(moved) + number],
        )
        for h in range(heads)
        for number, (source, landing) in enumerate(moved)
    )
    for copy in early + mine:
        copy.start()
    pl.semaphore_wait(barrier, frames - 1 + streams - 1)

    def remote(number, source, landing, offset, peer, slot):
        begin = pl.multiple_of(peer * local + offset, HEAD_DIM)
        return pltpu.make_async_remote_copy(
            src_ref=source.at[:, :, pl.ds(begin, landing.shape[2])],
            dst_ref=landing.at[pl.ds(slot * own, own)],
            send_sem=send_sems.at[number, peer],
            recv_sem=recv_sems.at[number, slot],
            device_id={"frame": peer},
        )

    def send_all(number, source, landing, offset):
        @pl.loop(1, frames)
        def _(i):
            peer = lax.rem(me + i, frames)
            remote(number, source, landing, offset, peer, me).start()

    def await_all(number, source, landing, offset):
        @pl.loop(1, frames)
        def _(i):
            peer = lax.rem(me + i, frames)
            remote(number, source, landing, offset, peer, peer).wait()

    last = heads * len(moved)
    for h in range(heads):
        for number, (source, landing) in enumerate(moved):
            send_all(h * len(moved) + number, source, landing[h], h * HEAD_DIM)

    def side_copies(part, source, landing):
        return [
            pltpu.make_async_remote_copy(
                src_ref=source,
                dst_ref=landing.at[my_stream],
                send_sem=side_send.at[part, i],
                recv_sem=side_recv.at[part, i],
                device_id={"stream": lax.rem(my_stream + i, streams)},
            )
            for i in range(1, streams)
        ]

    embed_copies = side_copies(0, embed_ref, embed_all)
    for copy in embed_copies:
        copy.start()
    embed_all[my_stream] = embed_ref[...]

    for copy in early:
        copy.wait()

    @pl.loop(0, frames)
    def _(i):
        columns = pl.ds(pl.multiple_of(i * local, local), local)
        for b in range(own):
            diff_own[b, :, columns] = (
                latent_own[b, :, columns].astype(jnp.float32)
                - target_own[b, :, columns].astype(jnp.float32)
            ).astype(jnp.bfloat16)

    my_diff = pltpu.make_async_copy(
        diff_own.at[:, :, pl.ds(me * local, local)],
        diff_in.at[pl.ds(me * own, own)],
        local_sems.at[3],
    )
    send_all(last, diff_own, diff_in, 0)
    my_diff.start()

    gate = lax.dot_general(
        embed_ref[...].astype(jnp.bfloat16),
        weight_own[...],
        (((1,), (1,)), ((), ())),
        preferred_element_type=jnp.float32,
    )

    @pl.loop(0, blocks)
    def _(t):
        found = jnp.int32(0)
        for b in range(blocks):
            found = jnp.where(order_ref[b] == t, b, found)
        place[t] = found

    for copy in mine:
        copy.wait()

    factor = math.log2(math.e) / math.sqrt(HEAD_DIM)
    ranges = math.gcd(groups, 4)
    for h in range(heads):
        lanes = slice(h * HEAD_DIM, (h + 1) * HEAD_DIM)
        for number, (source, landing) in enumerate(moved):
            await_all(h * len(moved) + number, source, landing[h], h * HEAD_DIM)

        @pl.loop(0, blocks)
        def _(t):
            rows = pl.ds(pl.multiple_of(t * block_len, block_len), block_len)
            key_sorted[rows, lanes] = key_in[h][place[t]]
            value_sorted[rows, lanes] = value_in[h][place[t]]

        for number in range(ranges):
            length = (number + 1) * (seq_len // ranges)

            @pl.loop(number * (groups // ranges), (number + 1) * (groups // ranges))
            def _(c):
                rows = jnp.concatenate(
                    [query_in[h][place[c * per_group + i]] for i in range(per_group)],
                    axis=0,
                )
                column_group = lax.broadcasted_iota(jnp.int32, (1, length), 1) // group_len
                bias = jnp.where(
                    (column_group >= start_ref[c]) & (column_group <= c), 0.0, HIDDEN
                ).astype(jnp.float32)
                scores = (
                    lax.dot_general(
                        rows,
                        key_sorted[:length, lanes],
                        (((1,), (1,)), ((), ())),
                        preferred_element_type=jnp.float32,
                    )
                    + bias
                )
                peak = jnp.max(scores, axis=-1, keepdims=True)
                unnorm = jnp.exp2((scores - peak) * factor)
                inverse = 1.0 / jnp.sum(unnorm, axis=-1, keepdims=True)
                probs = (unnorm * inverse).astype(jnp.bfloat16)
                attn = lax.dot_general(
                    probs,
                    value_sorted[:length, lanes],
                    (((1,), (0,)), ((), ())),
                    preferred_element_type=jnp.float32,
                ).astype(jnp.bfloat16)
                attn_all[pl.ds(c * per_group, per_group), :, lanes] = attn.reshape(
                    per_group, block_len, HEAD_DIM
                )
                wide = attn.astype(jnp.float32)
                squares[h, pl.ds(c, 1), :] = jnp.sum(wide * wide, axis=0, keepdims=True)

    base[...] = gate * jnp.concatenate([squares[h] for h in range(heads)], axis=1)

    def take(slot):
        for b in range(own):
            block = slot * own + b
            product = attn_all[order_ref[block]].astype(jnp.float32) * diff_in[block].astype(
                jnp.float32
            )
            partial[pl.ds(block, 1), :] = jnp.sum(product, axis=0, keepdims=True)

    my_diff.wait()
    take(me)

    @pl.loop(1, frames)
    def _(i):
        peer = lax.rem(me + frames - i, frames)
        remote(last, diff_own, diff_in, 0, peer, peer).wait_recv()
        take(peer)

    @pl.loop(0, groups)
    def _(c):
        total = base[pl.ds(c, 1), :]
        for i in range(per_group):
            total = total + partial[pl.ds(place[c * per_group + i], 1), :]
        sums_all[my_stream, pl.ds(c, 1), :] = total

    sum_copies = side_copies(1, sums_all.at[my_stream], sums_all)
    for copy in sum_copies:
        copy.start()
    for copy in embed_copies:
        copy.wait()
    for copy in sum_copies:
        copy.wait()

    @pl.loop(1, frames)
    def _(i):
        peer = lax.rem(me + i, frames)
        remote(last, diff_own, diff_in, 0, peer, me).wait_send()

    out_ref[...] = lax.dot_general(
        sums_all[...].reshape(streams * groups, local),
        embed_all[...].reshape(streams * groups, embed_ref.shape[1]),
        (((0,), (0,)), ((), ())),
        precision=lax.Precision.HIGHEST,
        preferred_element_type=jnp.float32,
    ) * (1.0 / math.sqrt(group_len))


def per_device(
    query, key, value, latent, target, noise_level, mod_weight, block_order, context_start
):
    frames = lax.axis_size("frame")
    streams = lax.axis_size("stream")
    tokens, width = query.shape[1:]
    local = width // frames
    blocks = block_order.shape[0]
    own = blocks // frames
    block_len = tokens // own
    groups = noise_level.shape[1]
    emb_width = mod_weight.shape[1]
    group_len = blocks // groups * block_len
    seq_len = blocks * block_len
    embed = sinusoid(noise_level[0], emb_width).astype(jnp.float32)
    bf16, f32 = jnp.bfloat16, jnp.float32
    shaped = [x.reshape(own, block_len, width) for x in (query, key, value, latent, target)]
    anywhere = pl.BlockSpec(memory_space=pl.ANY)
    scalars = pl.BlockSpec(memory_space=pltpu.SMEM)
    vectors = pl.BlockSpec(memory_space=pltpu.VMEM)
    heads = local // HEAD_DIM
    one_head = pltpu.VMEM((blocks, block_len, HEAD_DIM), bf16)
    landing = pltpu.VMEM((blocks, block_len, local), bf16)
    ordered = pltpu.VMEM((seq_len, local), bf16)
    held = pltpu.VMEM((own, block_len, width), bf16)
    return pl.pallas_call(
        functools.partial(kernel, frames, streams),
        out_shape=jax.ShapeDtypeStruct((local, emb_width), f32),
        in_specs=[scalars, scalars, vectors] + [anywhere] * 6,
        out_specs=vectors,
        scratch_shapes=[
            [one_head] * heads,
            [one_head] * heads,
            [one_head] * heads,
            landing,
            ordered,
            ordered,
            landing,
            held,
            held,
            held,
            pltpu.VMEM((local, emb_width), bf16),
            pltpu.VMEM((streams, groups, emb_width), f32),
            pltpu.VMEM((streams, groups, local), f32),
            pltpu.VMEM((heads, groups, HEAD_DIM), f32),
            pltpu.VMEM((groups, local), f32),
            pltpu.VMEM((blocks, local), f32),
            pltpu.SMEM((blocks,), jnp.int32),
            pltpu.SemaphoreType.DMA((3 * heads + 1, frames)),
            pltpu.SemaphoreType.DMA((3 * heads + 1, frames)),
            pltpu.SemaphoreType.DMA((2, streams)),
            pltpu.SemaphoreType.DMA((2, streams)),
            pltpu.SemaphoreType.DMA((4 + 3 * heads,)),
        ],
        compiler_params=pltpu.CompilerParams(
            collective_id=0, has_side_effects=True, vmem_limit_bytes=56 * 1024 * 1024
        ),
    )(block_order, context_start[0], embed, *shaped, mod_weight)


def solution(mesh):
    placed = (
        P("stream", "frame", None),
        P("stream", "frame", None),
        P("stream", "frame", None),
        P("stream", "frame", None),
        P("stream", "frame", None),
        P("stream", None),
        P(),
        P(),
        P("stream", None),
    )
    return jax.shard_map(
        per_device, mesh=mesh, in_specs=placed, out_specs=P("frame", None), check_vma=False
    )
```

time: 116 us -> 106 us (0.914); the launches traced: 116 us -> 104 us
  Pallas kernels: 113 us -> 101 us
    pallas_call x1, Pallas kernels: 113 us -> 101 us  [per_device(): pl.pallas_call(functools.partial(kernel, frames, streams), out_shape=jax....]
where the time goes in v1:
time: 106 us; the launch traced here: 104 us
  Pallas kernels  101 us (95%)
  local copies, waits for them, and re-layouts  1.67 us (2%)
  other arithmetic  1.4 us (1%)
    pallas_call x1, Pallas kernels, per_device(): pl.pallas_call(functools.partial(kernel, frames, streams), out_shape=jax....  101 us

profile of v1, /device:TPU:0, one launch (start us, length us, event | category | flops | bytes accessed | tf_op | source)
XLA Modules:
  0.0 104.3 jit_solution(6608470652748729644)
XLA Ops:
  0.0 0.7 multiply_bitcast_fusion
  0.7 0.1 fusion
  0.8 0.6 maximum_convert_fusion.embed_ref
  1.4 101.2 %shard_map.91 = f32[256,256]{1,0:T(8,128)} custom-call(s32[32]{0:T(128)} %order_ref.1, s32[16]{0:T(128)} %bitcast.13, f32[16,256]{1,0:T(8,128)} %maximum_convert_fusion.embed_ref, bf16[2,64,4096]{2,1,0:T(8,128)(2,1)} %bitcast.8, bf16[2,64,4096]{2,1,0:T(8,128)(2,1)} %bitcast.9, bf16[2,64,4096]{2,1,0:T(8,128)(2,1)} %bitcast.10, bf16[2,64,4096]{2,1,0:T(8,128)(2,1)} %bitcast.11, ...), custom_call_target="tpu_custom_call" | custom-call | tf_op jit(solution)/shard_map/pallas_call | solution.py:306
  102.6 1.7 %copy.11 = f32[256,256]{1,0:T(8,128)} copy(f32[256,256]{1,0:T(8,128)} %shard_map.91) | data formatting | bytes 524288
  (1 shorter events, 0.0 us)

commit v2 on v1

--- a/solution.py
+++ b/solution.py
@@ -12,19 +12,13 @@
 HIDDEN = -1e30
 
 
-def sinusoid(noise, emb_width):
-    half_width = emb_width // 2
-    frequency = jnp.exp(-math.log(10000.0) * jnp.arange(half_width, dtype=jnp.float32) / half_width)
-    angles = 1000.0 * noise[..., None] * frequency
-    return jnp.concatenate([jnp.cos(angles), jnp.sin(angles)], -1).astype(jnp.bfloat16)
-
-
 def kernel(
     frames,
     streams,
     order_ref,
     start_ref,
-    embed_ref,
+    noise_ref,
+    frequency_ref,
     query_ref,
     key_ref,
     value_ref,
@@ -60,7 +54,7 @@
     own, block_len, width = query_ref.shape
     local = width // frames
     blocks = diff_in.shape[0]
-    groups = embed_ref.shape[0]
+    groups = noise_ref.shape[0]
     per_group = blocks // groups
     group_len = per_group * block_len
     seq_len = blocks * block_len
@@ -137,10 +131,11 @@
             for i in range(1, streams)
         ]
 
-    embed_copies = side_copies(0, embed_ref, embed_all)
-    for copy in embed_copies:
-        copy.start()
-    embed_all[my_stream] = embed_ref[...]
+    half_width = frequency_ref.shape[1]
+    for c in range(groups):
+        angles = (1000.0 * noise_ref[c]) * frequency_ref[...]
+        waves = jnp.concatenate([jnp.cos(angles), jnp.sin(angles)], axis=1)
+        embed_all[my_stream, c : c + 1, :] = waves.astype(jnp.bfloat16).astype(jnp.float32)
 
     for copy in early:
         copy.wait()
@@ -163,7 +158,7 @@
     my_diff.start()
 
     gate = lax.dot_general(
-        embed_ref[...].astype(jnp.bfloat16),
+        embed_all[my_stream].astype(jnp.bfloat16),
         weight_own[...],
         (((1,), (1,)), ((), ())),
         preferred_element_type=jnp.float32,
@@ -240,6 +235,9 @@
             )
             partial[pl.ds(block, 1), :] = jnp.sum(product, axis=0, keepdims=True)
 
+    embed_copies = side_copies(0, embed_all.at[my_stream], embed_all)
+    for copy in embed_copies:
+        copy.start()
     my_diff.wait()
     take(me)
 
@@ -271,7 +269,7 @@
 
     out_ref[...] = lax.dot_general(
         sums_all[...].reshape(streams * groups, local),
-        embed_all[...].reshape(streams * groups, embed_ref.shape[1]),
+        embed_all[...].reshape(streams * groups, 2 * half_width),
         (((0,), (0,)), ((), ())),
         precision=lax.Precision.HIGHEST,
         preferred_element_type=jnp.float32,
@@ -292,7 +290,9 @@
     emb_width = mod_weight.shape[1]
     group_len = blocks // groups * block_len
     seq_len = blocks * block_len
-    embed = sinusoid(noise_level[0], emb_width).astype(jnp.float32)
+    half_width = emb_width // 2
+    exponents = jnp.arange(half_width, dtype=jnp.float32) / half_width
+    frequency = jnp.exp(-math.log(10000.0) * exponents)[None, :]
     bf16, f32 = jnp.bfloat16, jnp.float32
     shaped = [x.reshape(own, block_len, width) for x in (query, key, value, latent, target)]
     anywhere = pl.BlockSpec(memory_space=pl.ANY)
@@ -306,7 +306,7 @@
     return pl.pallas_call(
         functools.partial(kernel, frames, streams),
         out_shape=jax.ShapeDtypeStruct((local, emb_width), f32),
-        in_specs=[scalars, scalars, vectors] + [anywhere] * 6,
+        in_specs=[scalars, scalars, scalars, vectors] + [anywhere] * 6,
         out_specs=vectors,
         scratch_shapes=[
             [one_head] * heads,
@@ -335,7 +335,7 @@
         compiler_params=pltpu.CompilerParams(
             collective_id=0, has_side_effects=True, vmem_limit_bytes=56 * 1024 * 1024
         ),
-    )(block_order, context_start[0], embed, *shaped, mod_weight)
+    )(block_order, context_start[0], noise_level[0], frequency, *shaped, mod_weight)
 
 
 def solution(mesh):

time: 106 us -> 105 us (level)
  no operation moved by 1% of the time
where the time goes in v2:
time: 105 us; the launch traced here: 103 us
  Pallas kernels  101 us (96%)
  local copies, waits for them, and re-layouts  1.67 us (2%)
    pallas_call x1, Pallas kernels, per_device(): pl.pallas_call(functools.partial(kernel, frames, streams), out_shape=jax....  101 us

profile of v2, /device:TPU:0, one launch (start us, length us, event | category | flops | bytes accessed | tf_op | source)
XLA Modules:
  0.0 103.4 jit_solution(5187930265620072675)
XLA Ops:
  0.0 0.5 multiply_exponential_fusion.frequency_ref
  0.5 101.2 %shard_map.91 = f32[256,256]{1,0:T(8,128)} custom-call(s32[32]{0:T(128)} %order_ref.1, s32[16]{0:T(128)} %bitcast.12, f32[16]{0:T(128)} %bitcast.13, f32[1,128]{1,0:T(1,128)} %multiply_exponential_fusion.frequency_ref, bf16[2,64,4096]{2,1,0:T(8,128)(2,1)} %bitcast.7, bf16[2,64,4096]{2,1,0:T(8,128)(2,1)} %bitcast.8, bf16[2,64,4096]{2,1,0:T(8,128)(2,1)} %bitcast.9, ...), custom_call_target="tpu_custom_call" | custom-call | tf_op jit(solution)/shard_map/pallas_call | solution.py:306
  101.7 1.7 %copy.11 = f32[256,256]{1,0:T(8,128)} copy(f32[256,256]{1,0:T(8,128)} %shard_map.91) | data formatting | bytes 524288
